TPU v7x, 128 devices: a whole 4x4x4 slice. The times are simulated.
128 devices in a mesh: mem: 8 (over z_lo, y), sx: 4 (over z_hi, core), sy: 4 (over x).
Axes of the slice: x: 4, y: 4, z: 4 (z_hi: 2, z_lo: 2; z = z_hi * 2 + z_lo), core: 2. Of those that a mesh axis runs over, the one named last changes fastest.
Arguments:
- child: bfloat16 [32, 8, 192, 3072], P('mem', None, 'sx', 'sy'), may hold values from -13 to 13
Outputs:
- parent_mean: float32 [8, 64, 1024], P('mem', 'sx', 'sy')
- local_cov: float32 [64, 64, 1024], P('mem', 'sx', 'sy')
All inputs are finite; a program needn't handle non-finite values.
Results may differ from a plain program's by a relative error of at most 0.002.
Values sent between devices are 32-bit elements; how exact they have to be, the bound alone decides.
A program may use at most 192 MiB of HBM per device.

v0:
```python
import jax
import jax.numpy as jnp
import numpy as np
from jax import lax
from jax.sharding import Mesh
from jax.sharding import PartitionSpec as P

SX = ("sx_0", "sx_1")
MEM = ("mem_0", "mem_1")
MEM_SX_SY = ("mem_0", "mem_1", "sx_0", "sx_1", "sy")


def padded_2(array, sides, width):
    for axis, dim in sides:
        devices, length = (lax.axis_size(axis), array.shape[dim])
        up = [(i, (i + 1) % devices) for i in range(devices - 1)]
        down = [(j, i) for i, j in up]
        last = lax.slice_in_dim(array, length - width, length, axis=dim)
        initial = lax.slice_in_dim(array, 0, width, axis=dim)
        before = lax.ppermute(last, axis, up)
        after = lax.ppermute(initial, axis, down)
        array = jnp.concatenate([before, array, after], axis=dim)
    return array


def from_everyone(array, axis):
    copies = jnp.broadcast_to(array, (lax.axis_size(axis), *array.shape))
    return lax.all_to_all(copies, axis, split_axis=0, concat_axis=0, tiled=True)


def taken_together(array, axis):
    return from_everyone(array, axis).sum(axis=0)


def cut_along(array, dim, devices):
    shape = array.shape
    pieces = array.reshape(*shape[:dim], devices, shape[dim] // devices, *shape[dim + 1 :])
    return jnp.moveaxis(pieces, dim, 0)


def sum_at_owner(array, axis, dim):
    devices = lax.axis_size(axis)
    pieces = lax.all_to_all(cut_along(array, dim, devices), axis, 0, 0, tiled=True)
    return jnp.sum(pieces, axis=0)


def one_axis_at_a_time(array, axes):
    for axis in axes:
        array = lax.psum(array, axis)
    return array


def gaspari_table(reach):
    offsets = np.arange(-reach, reach + 1) * 1.0
    dist = np.sqrt(offsets[:, None] ** 2 + offsets[None, :] ** 2) / 2.5
    near = -0.25 * dist**5 + 0.5 * dist**4 + 0.625 * dist**3 - 5.0 / 3.0 * dist**2 + 1.0
    safe = np.maximum(dist, 0.001)
    far = (
        dist**5 / 12.0
        - 0.5 * dist**4
        + 0.625 * dist**3
        + 5.0 / 3.0 * dist**2
        - 5.0 * dist
        + 4.0
        - 2.0 / (3.0 * safe)
    )
    table = np.where(dist <= 1.0, near, np.where(dist < 2.0, far, 0.0))
    return table / table.sum()


def localize(owned, rows_dev, cols_dev):
    reach = 4
    padded = padded_2(owned, ((SX, 1), ("sy", 2)), reach)
    table = gaspari_table(reach)
    smoothed = jnp.zeros((owned.shape[0], rows_dev, cols_dev), jnp.float32)
    for first in range(2 * reach + 1):
        for second_off in range(2 * reach + 1):
            weight = float(table[first, second_off])
            if weight != 0.0:
                smoothed = (
                    smoothed
                    + weight
                    * padded[:, first : first + rows_dev, second_off : second_off + cols_dev]
                )
    return smoothed


def local(child):
    members_dev, levels, child_rows, child_cols = child.shape
    rows_dev = child_rows // 3
    cols_dev = child_cols // 3
    groups = lax.axis_size(MEM)
    members = members_dev * groups
    pairs_dev = levels * levels // groups
    level_dev = levels // groups
    device = lax.axis_index(MEM)
    parent = (
        jnp.sum(
            child.reshape(members_dev, levels, rows_dev, 3, cols_dev, 3),
            axis=(3, 5),
            dtype=jnp.float32,
        )
        / 9.0
    )
    totals = taken_together(jnp.sum(parent, axis=0), MEM)
    first_pair = device * pairs_dev
    pair_ids = first_pair + jnp.arange(pairs_dev, dtype=jnp.int32)
    diag_mask = (pair_ids // levels == pair_ids % levels).astype(jnp.float32)
    own_left = pair_ids // levels
    own_right = pair_ids % levels
    products = jnp.einsum("alxy,akxy->lkxy", parent, parent).reshape(
        levels * levels, rows_dev, cols_dev
    )
    second = sum_at_owner(products, MEM, 0)
    parent_mean = totals / members
    outer_own = jnp.take(parent_mean, own_left, axis=0) * jnp.take(parent_mean, own_right, axis=0)
    owned = (second - members * outer_own) / (members - 1)
    variance_total = one_axis_at_a_time(jnp.sum(owned * diag_mask[:, None, None]), MEM_SX_SY)
    cells = levels * rows_dev * lax.axis_size(SX) * cols_dev * lax.axis_size("sy")
    spread = variance_total / cells
    smoothed = localize(owned, rows_dev, cols_dev)
    local_cov = smoothed / (spread + 1e-06)
    mean_rows = lax.dynamic_slice_in_dim(parent_mean, device * level_dev, level_dev, 0)
    return (mean_rows, local_cov)


def solution(mesh):
    split = Mesh(
        mesh.devices.reshape(2, 4, 2, 2, mesh.shape["sy"]), ("mem_0", "mem_1", "sx_0", "sx_1", "sy")
    )
    in_specs = (P(MEM, None, SX, "sy"),)
    out_specs = (P(MEM, SX, "sy"), P(MEM, SX, "sy"))
    return jax.shard_map(local, mesh=split, in_specs=in_specs, out_specs=out_specs, check_vma=False)
```

profile of v0, /device:TPU:0, one launch (start us, length us, event | category | flops | bytes accessed | tf_op | source)
XLA Modules:
  0.0 194.3 jit_solution(8991469457047343743)
XLA Ops:
  0.6 37.3 %copy.9 = f32[4,8,48,768]{1,0,3,2:T(4,128)} copy(bf16[4,8,48,768]{3,2,1,0:T(8,128)(2,1)} %param.3) | data formatting | bytes 7077888 | tf_op jit(solution)/shard_map/convert_element_type | solution.py:98
  37.9 42.6 %reduce_sum.45 = f32[4,8,16,256]{1,0,3,2:T(4,128)} reduce(f32[4,8,16,3,256,3]{1,0,5,4,3,2:T(4,128)} %bitcast, f32[]{:T(128)} %constant.74.clone.1), dimensions={3,5}, to_apply=%region_0.0 | reduce | flops 1048576 | bytes 5242884 | tf_op jit(solution)/shard_map/reduce_sum | solution.py:98
  80.5 10.0 %multiply_reduce_fusion = f32[8,16,256]{0,2,1:T(8,128)S(1)} fusion(f32[4,8,16,256]{1,0,3,2:T(4,128)} %reduce_sum.45), kind=kLoop, calls=%fused_computation.4 | loop fusion | flops 229376 | bytes 655360 | tf_op jit(solution)/shard_map/reduce_sum | solution.py:105
  90.6 0.6 copy.10
  91.1 1.1 broadcast_in_dim.13
  92.3 5.9 %all-to-all-start = ((f32[8,8,16,256]{3,2,1,0:T(8,128)}), f32[8,8,16,256]{3,2,1,0:T(8,128)S(1)}, u32[]{:S(2)}, u32[]{:S(2)}) async-start(f32[8,8,16,256]{3,2,1,0:T(8,128)} %broadcast_in_dim.13), calls=%async_computation | async-start | bytes 2097152 | tf_op jit(solution)/shard_map/all_to_all | solution.py:28
  98.2 14.8 %convolution_bitcast_fusion = f32[8,8,16,256]{0,1,3,2:T(8,128)} fusion(f32[4,8,16,256]{1,0,3,2:T(4,128)} %reduce_sum.45), kind=kOutput, calls=%fused_computation.2 | convolution fusion | flops 2228224 | bytes 1572864 | tf_op jit(solution)/shard_map/alxy,akxy->lkxy/dot_general | solution.py:111
  113.0 9.1 %copy.11 = f32[8,8,16,256]{3,2,1,0:T(8,128)} copy(f32[8,8,16,256]{0,1,3,2:T(8,128)} %convolution_bitcast_fusion) | data formatting | bytes 2097152 | tf_op jit(solution)/shard_map/alxy,akxy->lkxy/transpose | solution.py:111
  122.2 5.7 %all-to-all-start.1 = ((f32[8,8,16,256]{3,2,1,0:T(8,128)}), f32[8,8,16,256]{3,2,1,0:T(8,128)S(1)}, u32[]{:S(2)}, u32[]{:S(2)}) async-start(f32[8,8,16,256]{3,2,1,0:T(8,128)} %copy.11), calls=%async_computation.1 | async-start | bytes 2097152 | tf_op jit(solution)/shard_map/all_to_all | solution.py:43
  128.0 0.6 gather_fusion.1
  128.6 0.6 gather_fusion
  129.2 13.8 %all-to-all-done.1 = f32[8,8,16,256]{3,2,1,0:T(8,128)S(1)} async-done(((f32[8,8,16,256]{3,2,1,0:T(8,128)}), f32[8,8,16,256]{3,2,1,0:T(8,128)S(1)}, u32[]{:S(2)}, u32[]{:S(2)}) %all-to-all-start.1) | async-done | bytes 1048608 | tf_op jit(solution)/shard_map/all_to_all | solution.py:43
  143.1 0.7 multiply_reduce_fusion.1
  143.8 1.3 collective-permute-start.1
  145.1 3.0 %collective-permute-start = (f32[8,4,256]{2,1,0:T(4,128)S(1)}, f32[8,4,256]{2,1,0:T(4,128)S(1)}, u32[]{:S(2)}, u32[]{:S(2)}) collective-permute-start(f32[8,4,256]{2,1,0:T(4,128)S(1)} %get-tuple-element.9), channel_id=1, source_target_pairs={{0,4},{4,8},{8,12},{1,5},{5,9},{9,13},{2,6},{6,10},{10,14},{3,7},{... | collective-permute-start | bytes 98312 | tf_op jit(solution)/shard_map/ppermute | solution.py:20
  148.2 5.6 %psum.35 = f32[]{:T(128)} all-reduce(f32[]{:T(128)} %get-tuple-element.3), channel_id=1, replica_groups=mesh['mem_0'=2,'mem_1'=4,'sx_0'=2,'sx_1'=2,'sy'=4] {'mem_0'}, use_global_device_ids=true, to_apply=%region_5.7 | all-reduce | flops 1 | bytes 8 | tf_op jit(solution)/shard_map/psum | solution.py:49
  153.7 9.2 %psum.36 = f32[]{:T(128)} all-reduce(f32[]{:T(128)} %psum.35), channel_id=1, replica_groups=mesh['mem_0'=2,'mem_1'=4,'sx_0'=2,'sx_1'=2,'sy'=4] {'mem_1'}, use_global_device_ids=true, to_apply=%region_6.8 | all-reduce | flops 1 | bytes 8 | tf_op jit(solution)/shard_map/psum | solution.py:49
  162.9 7.1 %psum.37 = f32[]{:T(128)} all-reduce(f32[]{:T(128)} %psum.36), channel_id=1, replica_groups=mesh['mem_0'=2,'mem_1'=4,'sx_0'=2,'sx_1'=2,'sy'=4] {'sx_0'}, use_global_device_ids=true, to_apply=%region_7.9 | all-reduce | flops 1 | bytes 8 | tf_op jit(solution)/shard_map/psum | solution.py:49
  170.0 3.1 %psum.38 = f32[]{:T(128)} all-reduce(f32[]{:T(128)} %psum.37), channel_id=1, replica_groups=mesh['mem_0'=2,'mem_1'=4,'sx_0'=2,'sx_1'=2,'sy'=4] {'sx_1'}, use_global_device_ids=true, to_apply=%region_8.10 | all-reduce | flops 1 | bytes 8 | tf_op jit(solution)/shard_map/psum | solution.py:49
  173.2 3.4 %collective-permute-start.2 = (f32[8,24,4]{2,1,0:T(8,128)S(1)}, f32[8,24,4]{2,1,0:T(8,128)S(1)}, u32[]{:S(2)}, u32[]{:S(2)}) collective-permute-start(f32[8,24,4]{2,1,0:T(8,128)S(1)} %get-tuple-element.7), channel_id=1, source_target_pairs={{0,1},{1,2},{2,3},{4,5},{5,6},{6,7},{8,9},{9,10},{10,11},{12,13},{... | collective-permute-start | bytes 9224 | tf_op jit(solution)/shard_map/ppermute | solution.py:20
  176.7 1.3 collective-permute-start.3
  178.0 0.6 constant_dynamic-slice_fusion
  178.6 12.2 %psum.39 = f32[]{:T(128)} all-reduce(f32[]{:T(128)} %psum.38), channel_id=1, replica_groups=mesh['mem_0'=2,'mem_1'=4,'sx_0'=2,'sx_1'=2,'sy'=4] {'sy'}, use_global_device_ids=true, to_apply=%region_9.11 | all-reduce | flops 1 | bytes 8 | tf_op jit(solution)/shard_map/psum | solution.py:49
  191.7 2.6 %fusion.13 = f32[8,16,256]{2,1,0:T(8,128)} fusion(f32[8,16,256]{2,1,0:T(8,128)S(1)} %broadcast_multiply_fusion, f32[8,4,256]{2,1,0:T(4,128)S(1)} %collective-permute-done.1, f32[8,24,260]{2,1,0:T(8,128)S(1)} %get-tuple-element.6, f32[8,24,260]{2,1,0:T(8,128)S(1)} %get-tuple-element.5, f32[8,4,256]{2,1,0:T(4,128)S(1)} %collective-permute-done, ...), kind=kLoop, calls=%fused_computation.32 | loop fusion | flops 4784128 | bytes 8323076 | tf_op jit(solution)/shard_map/div | solution.py:122
  (18 shorter events, 0.6 us)
Async XLA Ops:
  92.3 29.9 %all-to-all-start = ((f32[8,8,16,256]{3,2,1,0:T(8,128)}), f32[8,8,16,256]{3,2,1,0:T(8,128)S(1)}, u32[]{:S(2)}, u32[]{:S(2)}) async-start(f32[8,8,16,256]{3,2,1,0:T(8,128)} %broadcast_in_dim.13), calls=%async_computation | async-start | bytes 2097152 | tf_op jit(solution)/shard_map/all_to_all | solution.py:28
  122.2 20.8 %all-to-all-start.1 = ((f32[8,8,16,256]{3,2,1,0:T(8,128)}), f32[8,8,16,256]{3,2,1,0:T(8,128)S(1)}, u32[]{:S(2)}, u32[]{:S(2)}) async-start(f32[8,8,16,256]{3,2,1,0:T(8,128)} %copy.11), calls=%async_computation.1 | async-start | bytes 2097152 | tf_op jit(solution)/shard_map/all_to_all | solution.py:43
  143.8 29.3 %collective-permute-start.1 = (f32[8,4,256]{2,1,0:T(4,128)S(1)}, f32[8,4,256]{2,1,0:T(4,128)S(1)}, u32[]{:S(2)}, u32[]{:S(2)}) collective-permute-start(f32[8,4,256]{2,1,0:T(4,128)S(1)} %get-tuple-element.10), channel_id=1, source_target_pairs={{4,0},{8,4},{12,8},{5,1},{9,5},{13,9},{6,2},{10,6},{14,10},{7,3},{... | collective-permute-start | bytes 98312 | tf_op jit(solution)/shard_map/ppermute | solution.py:21
  145.1 28.0 %collective-permute-start = (f32[8,4,256]{2,1,0:T(4,128)S(1)}, f32[8,4,256]{2,1,0:T(4,128)S(1)}, u32[]{:S(2)}, u32[]{:S(2)}) collective-permute-start(f32[8,4,256]{2,1,0:T(4,128)S(1)} %get-tuple-element.9), channel_id=1, source_target_pairs={{0,4},{4,8},{8,12},{1,5},{5,9},{9,13},{2,6},{6,10},{10,14},{3,7},{... | collective-permute-start | bytes 98312 | tf_op jit(solution)/shard_map/ppermute | solution.py:20
  173.2 18.2 %collective-permute-start.2 = (f32[8,24,4]{2,1,0:T(8,128)S(1)}, f32[8,24,4]{2,1,0:T(8,128)S(1)}, u32[]{:S(2)}, u32[]{:S(2)}) collective-permute-start(f32[8,24,4]{2,1,0:T(8,128)S(1)} %get-tuple-element.7), channel_id=1, source_target_pairs={{0,1},{1,2},{2,3},{4,5},{5,6},{6,7},{8,9},{9,10},{10,11},{12,13},{... | collective-permute-start | bytes 9224 | tf_op jit(solution)/shard_map/ppermute | solution.py:20
  176.7 14.8 %collective-permute-start.3 = (f32[8,24,4]{2,1,0:T(8,128)S(1)}, f32[8,24,4]{2,1,0:T(8,128)S(1)}, u32[]{:S(2)}, u32[]{:S(2)}) collective-permute-start(f32[8,24,4]{2,1,0:T(8,128)S(1)} %get-tuple-element.8), channel_id=1, source_target_pairs={{1,0},{2,1},{3,2},{5,4},{6,5},{7,6},{9,8},{10,9},{11,10},{13,12},{... | collective-permute-start | bytes 9224 | tf_op jit(solution)/shard_map/ppermute | solution.py:21
where the time goes:
time: 196 us; the launch traced here: 194 us
  other arithmetic  56.4 us (29%)
  local copies, waits for them, and re-layouts  50 us (26%)
  blocking collectives  37.2 us (19%)
  starting transfers between devices  20.6 us (11%)
  matrix products  14.8 us (8%)
  waiting for transfers between devices  13.8 us (7%)
    reduce_sum x1, other arithmetic, local(): jnp.sum(child.reshape(members_dev, levels, rows_dev, 3, cols_dev, 3), axi...  42.6 us
    convert_element_type x1, local copies, waits for them, and re-layouts, local(): jnp.sum(child.reshape(members_dev, levels, rows_dev, 3, cols_dev, 3), axi...  37.3 us
    psum x5, blocking collectives, one_axis_at_a_time(): array = lax.psum(array, axis)  37.2 us
    dot_general x1, matrix products, local(): jnp.einsum('alxy,akxy->lkxy', parent, parent)  14.8 us
    all_to_all x1, waiting for transfers between devices, sum_at_owner(): lax.all_to_all(cut_along(array, dim, devices), axis, 0, 0, tiled=True)  13.8 us
    reduce_sum x1, other arithmetic, local(): totals = taken_together(jnp.sum(parent, axis=0), MEM)  10 us
    transpose x1, local copies, waits for them, and re-layouts, local(): jnp.einsum('alxy,akxy->lkxy', parent, parent)  9.14 us
    ppermute x2, starting transfers between devices, padded_2(): before = lax.ppermute(last, axis, up)  6.43 us
  transfers between devices with their start and end apart: 6, of which 1 were waited for; matrix products, arithmetic and copies ran while one was open for 13% of the time, Pallas kernels for 0%

commit v1 on v0

--- a/solution.py
+++ b/solution.py
@@ -46,7 +46,12 @@
 
 def one_axis_at_a_time(array, axes):
     for axis in axes:
-        array = lax.psum(array, axis)
+
+        def _obtain_stops_all(x0, along_axis):
+            w2 = lax.all_gather(x0, along_axis).sum(axis=0)
+            return w2
+
+        array = _obtain_stops_all(array, axis)
     return array
 
 

time: 196 us -> 206 us (1.051)
  local copies, waits for them, and re-layouts: 50 us -> 60.2 us
  blocking collectives: 37.2 us -> 34 us
  other arithmetic: 56.4 us -> 59.4 us
    psum x5 -> x0, blocking collectives: 37.2 us -> none  [one_axis_at_a_time(): array = lax.psum(array, axis)]
    unnamed x0 -> x5, blocking collectives: none -> 34 us
    unnamed x0 -> x25, local copies, waits for them, and re-layouts: none -> 10.2 us
    reduce_sum x0 -> x5, other arithmetic: none -> 3.02 us  [_obtain_stops_all(): w2 = lax.all_gather(x0, along_axis).sum(axis=0)]
  transfers between devices with their start and end apart: 6 -> 6, of which waited for: 1 -> 1; matrix products, arithmetic and copies ran while one was open for 13% -> 19% of each run, Pallas kernels for 0% -> 0%
where the time goes in v1:
time: 206 us; the launch traced here: 204 us
  local copies, waits for them, and re-layouts  60.2 us (29%)
  other arithmetic  59.4 us (29%)
  blocking collectives  34 us (17%)
  starting transfers between devices  20.6 us (10%)
  matrix products  14.8 us (7%)
  waiting for transfers between devices  13.8 us (7%)
    reduce_sum x1, other arithmetic, local(): jnp.sum(child.reshape(members_dev, levels, rows_dev, 3, cols_dev, 3), axi...  42.6 us
    convert_element_type x1, local copies, waits for them, and re-layouts, local(): jnp.sum(child.reshape(members_dev, levels, rows_dev, 3, cols_dev, 3), axi...  37.3 us
    unnamed x5, blocking collectives  34 us
    dot_general x1, matrix products, local(): jnp.einsum('alxy,akxy->lkxy', parent, parent)  14.8 us
    all_to_all x1, waiting for transfers between devices, sum_at_owner(): lax.all_to_all(cut_along(array, dim, devices), axis, 0, 0, tiled=True)  13.8 us
    unnamed x25, local copies, waits for them, and re-layouts  10.2 us
    reduce_sum x1, other arithmetic, local(): totals = taken_together(jnp.sum(parent, axis=0), MEM)  10 us
    transpose x1, local copies, waits for them, and re-layouts, local(): jnp.einsum('alxy,akxy->lkxy', parent, parent)  9.18 us
  transfers between devices with their start and end apart: 6, of which 1 were waited for; matrix products, arithmetic and copies ran while one was open for 19% of the time, Pallas kernels for 0%

profile of v1, /device:TPU:0, one launch (start us, length us, event | category | flops | bytes accessed | tf_op | source)
XLA Modules:
  0.0 204.4 jit_solution(1983263128387535381)
XLA Ops:
  0.6 37.3 %copy.9 = f32[4,8,48,768]{1,0,3,2:T(4,128)} copy(bf16[4,8,48,768]{3,2,1,0:T(8,128)(2,1)} %param.3) | data formatting | bytes 7077888 | tf_op jit(solution)/shard_map/convert_element_type | solution.py:103
  37.9 42.6 %reduce_sum.90 = f32[4,8,16,256]{1,0,3,2:T(4,128)} reduce(f32[4,8,16,3,256,3]{1,0,5,4,3,2:T(4,128)} %bitcast, f32[]{:T(128)} %constant.74.clone.1), dimensions={3,5}, to_apply=%region_0.0 | reduce | flops 1048576 | bytes 5242884 | tf_op jit(solution)/shard_map/reduce_sum | solution.py:103
  80.5 10.0 %multiply_reduce_fusion = f32[8,16,256]{0,2,1:T(8,128)S(1)} fusion(f32[4,8,16,256]{1,0,3,2:T(4,128)} %reduce_sum.90), kind=kLoop, calls=%fused_computation.4 | loop fusion | flops 229376 | bytes 655360 | tf_op jit(solution)/shard_map/reduce_sum | solution.py:110
  91.1 1.1 broadcast_in_dim.13
  92.3 5.9 %all-to-all-start = ((f32[8,8,16,256]{3,2,1,0:T(8,128)}), f32[8,8,16,256]{3,2,1,0:T(8,128)S(1)}, u32[]{:S(2)}, u32[]{:S(2)}) async-start(f32[8,8,16,256]{3,2,1,0:T(8,128)} %broadcast_in_dim.13), calls=%async_computation | async-start | bytes 2097152 | tf_op jit(solution)/shard_map/all_to_all | solution.py:28
  98.2 14.8 %convolution_bitcast_fusion = f32[8,8,16,256]{0,1,3,2:T(8,128)} fusion(f32[4,8,16,256]{1,0,3,2:T(4,128)} %reduce_sum.90), kind=kOutput, calls=%fused_computation.2 | convolution fusion | flops 2228224 | bytes 1572864 | tf_op jit(solution)/shard_map/alxy,akxy->lkxy/dot_general | solution.py:116
  113.0 9.2 %copy.11 = f32[8,8,16,256]{3,2,1,0:T(8,128)} copy(f32[8,8,16,256]{0,1,3,2:T(8,128)} %convolution_bitcast_fusion) | data formatting | bytes 2097152 | tf_op jit(solution)/shard_map/alxy,akxy->lkxy/transpose | solution.py:116
  122.2 5.7 %all-to-all-start.1 = ((f32[8,8,16,256]{3,2,1,0:T(8,128)}), f32[8,8,16,256]{3,2,1,0:T(8,128)S(1)}, u32[]{:S(2)}, u32[]{:S(2)}) async-start(f32[8,8,16,256]{3,2,1,0:T(8,128)} %copy.11), calls=%async_computation.1 | async-start | bytes 2097152 | tf_op jit(solution)/shard_map/all_to_all | solution.py:43
  129.2 13.8 %all-to-all-done.1 = f32[8,8,16,256]{3,2,1,0:T(8,128)S(1)} async-done(((f32[8,8,16,256]{3,2,1,0:T(8,128)}), f32[8,8,16,256]{3,2,1,0:T(8,128)S(1)}, u32[]{:S(2)}, u32[]{:S(2)}) %all-to-all-start.1) | async-done | bytes 1048608 | tf_op jit(solution)/shard_map/all_to_all | solution.py:43
  143.9 1.3 collective-permute-start.1
  145.2 3.0 %collective-permute-start = (f32[8,4,256]{2,1,0:T(4,128)S(1)}, f32[8,4,256]{2,1,0:T(4,128)S(1)}, u32[]{:S(2)}, u32[]{:S(2)}) collective-permute-start(f32[8,4,256]{2,1,0:T(4,128)S(1)} %get-tuple-element.9), channel_id=1, source_target_pairs={{0,4},{4,8},{8,12},{1,5},{5,9},{9,13},{2,6},{6,10},{10,14},{3,7},{... | collective-permute-start | bytes 98312 | tf_op jit(solution)/shard_map/ppermute | solution.py:20
  149.5 1.4 dynamic-update-slice
  151.5 4.9 %all-reduce = f32[2]{0:T(128)S(1)} all-reduce(f32[2]{0:T(128)S(1)} %dynamic-update-slice), channel_id=1, replica_groups=mesh['mem_0'=2,'mem_1'=4,'sx_0'=2,'sx_1'=2,'sy'=4] {'mem_0'}, use_global_device_ids=true, to_apply=%add | all-reduce | flops 2 | bytes 16
  157.0 1.4 dynamic-update-slice.1
  159.1 8.6 %all-reduce.1 = f32[4]{0:T(128)S(1)} all-reduce(f32[4]{0:T(128)S(1)} %dynamic-update-slice.1), channel_id=1, replica_groups=mesh['mem_0'=2,'mem_1'=4,'sx_0'=2,'sx_1'=2,'sy'=4] {'mem_1'}, use_global_device_ids=true, to_apply=%add.1 | all-reduce | flops 4 | bytes 32
  168.3 1.4 dynamic-update-slice.2
  170.3 6.5 %all-reduce.2 = f32[2]{0:T(128)S(1)} all-reduce(f32[2]{0:T(128)S(1)} %dynamic-update-slice.2), channel_id=1, replica_groups=mesh['mem_0'=2,'mem_1'=4,'sx_0'=2,'sx_1'=2,'sy'=4] {'sx_0'}, use_global_device_ids=true, to_apply=%add.2 | all-reduce | flops 2 | bytes 16
  177.4 1.4 dynamic-update-slice.3
  178.8 2.4 %all-reduce.3 = f32[2]{0:T(128)S(1)} all-reduce(f32[2]{0:T(128)S(1)} %dynamic-update-slice.3), channel_id=1, replica_groups=mesh['mem_0'=2,'mem_1'=4,'sx_0'=2,'sx_1'=2,'sy'=4] {'sx_1'}, use_global_device_ids=true, to_apply=%add.3 | all-reduce | flops 2 | bytes 16
  181.8 1.4 dynamic-update-slice.4
  183.4 3.4 %collective-permute-start.2 = (f32[8,24,4]{2,1,0:T(8,128)S(1)}, f32[8,24,4]{2,1,0:T(8,128)S(1)}, u32[]{:S(2)}, u32[]{:S(2)}) collective-permute-start(f32[8,24,4]{2,1,0:T(8,128)S(1)} %get-tuple-element.7), channel_id=1, source_target_pairs={{0,1},{1,2},{2,3},{4,5},{5,6},{6,7},{8,9},{9,10},{10,11},{12,13},{... | collective-permute-start | bytes 9224 | tf_op jit(solution)/shard_map/ppermute | solution.py:20
  186.8 1.3 collective-permute-start.3
  188.7 11.6 %all-reduce.4 = f32[4]{0:T(128)S(1)} all-reduce(f32[4]{0:T(128)S(1)} %dynamic-update-slice.4), channel_id=1, replica_groups=mesh['mem_0'=2,'mem_1'=4,'sx_0'=2,'sx_1'=2,'sy'=4] {'sy'}, use_global_device_ids=true, to_apply=%add.4 | all-reduce | flops 4 | bytes 32
  201.8 2.6 %fusion.13 = f32[8,16,256]{2,1,0:T(8,128)} fusion(f32[8,16,256]{2,1,0:T(8,128)S(1)} %broadcast_multiply_fusion, f32[8,4,256]{2,1,0:T(4,128)S(1)} %collective-permute-done.1, f32[8,24,260]{2,1,0:T(8,128)S(1)} %get-tuple-element.6, f32[8,24,260]{2,1,0:T(8,128)S(1)} %get-tuple-element.5, f32[8,4,256]{2,1,0:T(4,128)S(1)} %collective-permute-done, ...), kind=kLoop, calls=%fused_computation.32 | loop fusion | flops 4784128 | bytes 8323076 | tf_op jit(solution)/shard_map/div | solution.py:127
  (48 shorter events, 9.7 us)
Async XLA Ops:
  92.3 30.0 %all-to-all-start = ((f32[8,8,16,256]{3,2,1,0:T(8,128)}), f32[8,8,16,256]{3,2,1,0:T(8,128)S(1)}, u32[]{:S(2)}, u32[]{:S(2)}) async-start(f32[8,8,16,256]{3,2,1,0:T(8,128)} %broadcast_in_dim.13), calls=%async_computation | async-start | bytes 2097152 | tf_op jit(solution)/shard_map/all_to_all | solution.py:28
  113.0 35.3 %copy-start.4 = (u32[128]{0:T(128)S(1)}, u32[128]{0:T(128)}, u32[]{:S(2)}) copy-start(u32[128]{0:T(128)} %constant.108) | copy-start | bytes 1540
  113.0 35.8 %copy-start.3 = (u32[128]{0:T(128)S(1)}, u32[128]{0:T(128)}, u32[]{:S(2)}) copy-start(u32[128]{0:T(128)} %constant.113) | copy-start | bytes 1540
  113.0 37.9 %copy-start.2 = (u32[128]{0:T(128)S(1)}, u32[128]{0:T(128)}, u32[]{:S(2)}) copy-start(u32[128]{0:T(128)} %constant.118) | copy-start | bytes 1540
  113.0 45.5 %copy-start.1 = (u32[128]{0:T(128)S(1)}, u32[128]{0:T(128)}, u32[]{:S(2)}) copy-start(u32[128]{0:T(128)} %constant.123) | copy-start | bytes 1540
  113.0 56.7 %copy-start = (u32[128]{0:T(128)S(1)}, u32[128]{0:T(128)}, u32[]{:S(2)}) copy-start(u32[128]{0:T(128)} %constant.128) | copy-start | bytes 1540
  122.2 20.8 %all-to-all-start.1 = ((f32[8,8,16,256]{3,2,1,0:T(8,128)}), f32[8,8,16,256]{3,2,1,0:T(8,128)S(1)}, u32[]{:S(2)}, u32[]{:S(2)}) async-start(f32[8,8,16,256]{3,2,1,0:T(8,128)} %copy.11), calls=%async_computation.1 | async-start | bytes 2097152 | tf_op jit(solution)/shard_map/all_to_all | solution.py:43
  143.9 39.3 %collective-permute-start.1 = (f32[8,4,256]{2,1,0:T(4,128)S(1)}, f32[8,4,256]{2,1,0:T(4,128)S(1)}, u32[]{:S(2)}, u32[]{:S(2)}) collective-permute-start(f32[8,4,256]{2,1,0:T(4,128)S(1)} %get-tuple-element.10), channel_id=1, source_target_pairs={{4,0},{8,4},{12,8},{5,1},{9,5},{13,9},{6,2},{10,6},{14,10},{7,3},{... | collective-permute-start | bytes 98312 | tf_op jit(solution)/shard_map/ppermute | solution.py:21
  145.2 38.0 %collective-permute-start = (f32[8,4,256]{2,1,0:T(4,128)S(1)}, f32[8,4,256]{2,1,0:T(4,128)S(1)}, u32[]{:S(2)}, u32[]{:S(2)}) collective-permute-start(f32[8,4,256]{2,1,0:T(4,128)S(1)} %get-tuple-element.9), channel_id=1, source_target_pairs={{0,4},{4,8},{8,12},{1,5},{5,9},{9,13},{2,6},{6,10},{10,14},{3,7},{... | collective-permute-start | bytes 98312 | tf_op jit(solution)/shard_map/ppermute | solution.py:20
  183.4 18.2 %collective-permute-start.2 = (f32[8,24,4]{2,1,0:T(8,128)S(1)}, f32[8,24,4]{2,1,0:T(8,128)S(1)}, u32[]{:S(2)}, u32[]{:S(2)}) collective-permute-start(f32[8,24,4]{2,1,0:T(8,128)S(1)} %get-tuple-element.7), channel_id=1, source_target_pairs={{0,1},{1,2},{2,3},{4,5},{5,6},{6,7},{8,9},{9,10},{10,11},{12,13},{... | collective-permute-start | bytes 9224 | tf_op jit(solution)/shard_map/ppermute | solution.py:20
  186.8 14.8 %collective-permute-start.3 = (f32[8,24,4]{2,1,0:T(8,128)S(1)}, f32[8,24,4]{2,1,0:T(8,128)S(1)}, u32[]{:S(2)}, u32[]{:S(2)}) collective-permute-start(f32[8,24,4]{2,1,0:T(8,128)S(1)} %get-tuple-element.8), channel_id=1, source_target_pairs={{1,0},{2,1},{3,2},{5,4},{6,5},{7,6},{9,8},{10,9},{11,10},{13,12},{... | collective-permute-start | bytes 9224 | tf_op jit(solution)/shard_map/ppermute | solution.py:21
